TPU v7x, 32 devices: a whole 2x2x4 slice. The times are simulated.
32 devices in a mesh: up: 8 (over y, x, core), dn: 4 (over z).
Axes of the slice: x: 2, y: 2, z: 4, core: 2. Of those that a mesh axis runs over, the one named last changes fastest.
Arguments:
- start_vector: bfloat16 [13312, 13312], P('up', 'dn'), may hold values from -6 to 6
- hop_tiles: bfloat16 [104, 5, 128, 128], replicated, may hold values from -0.5 to 0.5
- tile_columns: int32 [104, 5], replicated, may hold values from 0 to 103, as said below
- tile_signs: int32 [104, 5], replicated, may hold values from 0 to 1
- occupation: int32 [16, 13312], replicated, may hold values from 0 to 1, as said below
Outputs:
- next_vector: bfloat16 [13312, 13312], P('up', 'dn')
- alphas: float32 [2], replicated
- betas: float32 [2], replicated
Inputs may be any that keep to these rules, and one draw needn't show every extreme that they name: Each row of tile_columns names 5 different tile columns. Every column of occupation holds exactly 8 ones.
All inputs are finite; a program needn't handle non-finite values.
Results may differ from a plain program's by a relative error of at most 0.0065.
Values may be sent and summed in bfloat16 or wider, within the bound.
A program may use at most 256 MiB of HBM per device.

v0:
```python
import functools

import jax
import jax.numpy as jnp
from jax import lax
from jax.experimental import pallas as pl
from jax.experimental.pallas import tpu as pltpu
from jax.sharding import PartitionSpec as P

STEPS = 2


coupling = 4.0


def hop_kernel(tile_k, tile, group, parts_tiles, columns_ref, x_ref, tiles_ref, out_ref):
    first = pl.program_id(0) * group

    def one_tile(t, carry):
        picked = []
        for k in range(tile_k):
            column = columns_ref[(first + t) * tile_k + k]
            at = pl.multiple_of(lax.rem(column, parts_tiles) * tile, tile)
            picked.append(x_ref[lax.div(column, parts_tiles), :, pl.ds(at, tile)])
        left = jnp.concatenate(picked, axis=1)
        result = jnp.dot(left, tiles_ref[t], preferred_element_type=jnp.float32)
        out_ref[0, :, pl.ds(pl.multiple_of(t * tile, tile), tile)] = result.astype(jnp.bfloat16)
        return carry

    lax.fori_loop(0, group, one_tile, 0)


def hop_blocks(x, stacked, columns, tile_k):
    parts, rows, width = x.shape
    tiles, depth, tile = stacked.shape
    if width % tile:
        joined = x.transpose(1, 0, 2).reshape(1, rows, parts * width)
        hopped = hop_blocks(joined, stacked, columns, tile_k)
        return hopped.reshape(rows, parts, width).transpose(1, 0, 2)
    parts_tiles = width // tile
    group = max(d for d in range(1, 17) if parts_tiles % d == 0)
    per_part = parts_tiles // group
    return pl.pallas_call(
        functools.partial(hop_kernel, tile_k, tile, group, parts_tiles),
        grid_spec=pltpu.PrefetchScalarGridSpec(
            num_scalar_prefetch=1,
            grid=(tiles // group,),
            in_specs=[
                pl.BlockSpec((parts, rows, width), lambda i, c: (0, 0, 0)),
                pl.BlockSpec((group, depth, tile), lambda i, c: (i, 0, 0)),
            ],
            out_specs=pl.BlockSpec(
                (1, rows, group * tile), lambda i, c: (i // per_part, 0, i % per_part)
            ),
        ),
        out_shape=jax.ShapeDtypeStruct(x.shape, jnp.bfloat16),
        compiler_params=pltpu.CompilerParams(vmem_limit_bytes=56 * 1024 * 1024),
        cost_estimate=pl.CostEstimate(
            flops=2 * rows * tiles * depth * tile,
            bytes_accessed=4 * rows * parts * width + 2 * tiles * depth * tile,
            transcendentals=0,
        ),
    )(columns, x, stacked)


def body(start_vector, hop_tiles, tile_columns, tile_signs, occupation):
    tiles, tile_k, tile, _ = hop_tiles.shape
    signed = hop_tiles * (1 - 2 * tile_signs).astype(jnp.bfloat16)[:, :, None, None]
    stacked = signed.transpose(0, 1, 3, 2).reshape(tiles, tile_k * tile, tile)
    columns = tile_columns.reshape(-1)
    block_rows, block_cols = start_vector.shape
    count_up = lax.axis_size("up")
    count_down = lax.axis_size("dn")
    row_start = lax.axis_index("up") * block_rows
    col_start = lax.axis_index("dn") * block_cols
    occ_rows = lax.dynamic_slice_in_dim(occupation, row_start, block_rows, 1).astype(jnp.bfloat16)
    occ_cols = lax.dynamic_slice_in_dim(occupation, col_start, block_cols, 1).astype(jnp.bfloat16)
    diagonal = (
        coupling * jnp.einsum("sa,sb->ab", occ_rows, occ_cols, preferred_element_type=jnp.float32)
    ).astype(jnp.bfloat16)
    total = lax.psum(jnp.sum(jnp.square(start_vector.astype(jnp.float32))), ("up", "dn"))
    scale = 1.0 / jnp.maximum(jnp.sqrt(total), 1.0)
    vector = start_vector.astype(jnp.float32) * scale
    length = total / jnp.maximum(total, 1.0)
    previous = None
    beta_value = None
    alpha_list = []
    beta_list = []
    for iteration in range(STEPS):
        rounded = start_vector if iteration == 0 else vector.astype(jnp.bfloat16)
        down = rounded.reshape(count_down, block_rows // count_down, block_cols)
        up = rounded.T.reshape(count_up, block_cols // count_up, block_rows)
        down = lax.all_to_all(down, "dn", 0, 0, tiled=True)
        up = lax.all_to_all(up, "up", 0, 0, tiled=True)
        down = hop_blocks(down, stacked, columns, tile_k)
        down = lax.all_to_all(down, "dn", 0, 0, tiled=True)
        up = hop_blocks(up, stacked, columns, tile_k)
        up = lax.all_to_all(up, "up", 0, 0, tiled=True)
        hopped_down = down.reshape(block_rows, block_cols)
        hopped_up = up.reshape(block_cols, block_rows).T
        hopped = hopped_up.astype(jnp.float32) + hopped_down.astype(jnp.float32)
        if iteration == 0:
            work = hopped * scale + diagonal * vector
        else:
            work = hopped + diagonal * vector - beta_value * previous
        intersect, square = lax.psum((jnp.sum(work * vector), jnp.sum(work * work)), ("up", "dn"))
        work = work - intersect * vector
        residual = square - 2.0 * intersect * intersect + intersect * intersect * length
        beta_value = jnp.sqrt(jnp.maximum(residual, 1.0))
        length = residual / jnp.maximum(residual, 1.0)
        previous = vector
        vector = work / beta_value
        alpha_list.append(intersect)
        beta_list.append(beta_value)
    final = vector.astype(jnp.bfloat16)
    return (final, jnp.stack(alpha_list), jnp.stack(beta_list))


def solution(mesh):
    placed = (P("up", "dn"), P(), P(), P(), P())
    return jax.shard_map(
        body, mesh=mesh, in_specs=placed, out_specs=(P("up", "dn"), P(), P()), check_vma=False
    )
```

profile of v0, /device:TPU:0, one launch (start us, length us, event | category | flops | bytes accessed | tf_op | source)
XLA Modules:
  0.0 1784.6 jit_solution(8246984403498989128)
XLA Ops:
  0.6 17.2 copy.15
  17.8 0.0 copy-start.1
  17.9 0.0 copy-start
  17.9 129.8 %all_to_all.40.x_ref = bf16[8,416,1664]{2,1,0:T(8,128)(2,1)} all-to-all(bf16[8,416,1664]{2,1,0:T(8,128)(2,1)} %bitcast.53), channel_id=1, replica_groups=mesh['up'=8,'dn'=4] {'up'}, dimensions={0} | all-to-all | bytes 22151168 | tf_op jit(solution)/shard_map/all_to_all | solution.py:94
  147.6 6.1 all-to-all-start.2
  153.7 0.0 copy-done.1
  153.8 0.1 copy.16
  153.9 0.0 copy-done
  153.9 0.1 copy.14
  154.0 0.8 reshape.37.columns_ref
  154.8 14.1 multiply_bitcast_fusion
  168.9 22.7 %copy.17 = bf16[104,5,128,128]{3,2,1,0:T(8,128)(2,1)} copy(bf16[104,5,128,128]{2,3,1,0:T(8,128)(2,1)} %multiply_bitcast_fusion) | data formatting | bytes 34078720 | tf_op jit(solution)/shard_map/transpose | solution.py:69
  191.6 38.7 %shard_map.76 = bf16[8,416,1664]{2,1,0:T(8,128)(2,1)} custom-call(s32[520]{0:T(1024)} %reshape.37.columns_ref, bf16[8,416,1664]{2,1,0:T(8,128)(2,1)} %all_to_all.40.x_ref, bf16[104,640,128]{2,1,0:T(8,128)(2,1)} %bitcast.45), custom_call_target="tpu_custom_call" | custom-call | flops 7088373760 | bytes 39190528 | tf_op jit(solution)/shard_map/pallas_call | solution.py:43
  230.3 165.0 %all-to-all-done.2.x_ref = bf16[4,416,3328]{2,1,0:T(8,128)(2,1)} async-done(((bf16[4,416,3328]{2,1,0:T(8,128)(2,1)}), bf16[4,416,3328]{2,1,0:T(8,128)(2,1)}, u32[]{:S(2)}, u32[]{:S(2)}) %all-to-all-start.2) | async-done | bytes 11075616 | tf_op jit(solution)/shard_map/all_to_all | solution.py:93
  395.3 5.2 all-to-all-start.1
  400.5 38.9 %shard_map.77 = bf16[4,416,3328]{2,1,0:T(8,128)(2,1)} custom-call(s32[520]{0:T(1024)} %reshape.37.columns_ref, bf16[4,416,3328]{2,1,0:T(8,128)(2,1)} %all-to-all-done.2.x_ref, bf16[104,640,128]{2,1,0:T(8,128)(2,1)} %bitcast.46), custom_call_target="tpu_custom_call" | custom-call | flops 7088373760 | bytes 39190528 | tf_op jit(solution)/shard_map/pallas_call | solution.py:43
  439.4 83.9 %all-to-all-done.1 = bf16[8,416,1664]{2,1,0:T(8,128)(2,1)} async-done(((bf16[8,416,1664]{2,1,0:T(8,128)(2,1)}), bf16[8,416,1664]{2,1,0:T(8,128)(2,1)}, u32[]{:S(2)}, u32[]{:S(2)}) %all-to-all-start.1) | async-done | bytes 11075616 | tf_op jit(solution)/shard_map/all_to_all | solution.py:98
  523.3 6.1 all-to-all-start.3
  529.4 10.4 fusion.7
  539.8 248.8 %psum.35 = f32[]{:T(128)} all-reduce(f32[]{:T(128)} %fusion.7), channel_id=1, replica_groups=mesh['up'=8,'dn'=4] {'up','dn'}, use_global_device_ids=true, to_apply=%region_1.0 | all-reduce | flops 1 | bytes 8 | tf_op jit(solution)/shard_map/psum | solution.py:81
  790.7 12.2 bitcast_convert_fusion.1
  802.9 22.8 %copy.18 = f32[3328,1664]{0,1:T(8,128)} copy(f32[3328,1664]{1,0:T(8,128)} %bitcast_convert_fusion.1) | data formatting | bytes 44302336 | tf_op jit(solution)/shard_map/convert_element_type | solution.py:101
  825.7 0.0 all-to-all-done.3
  825.7 22.9 %fusion.3 = (f32[]{:T(128)}, f32[]{:T(128)}, bf16[1664,3328]{1,0:T(8,128)(2,1)}) fusion(bf16[1664,3328]{1,0:T(8,128)(2,1)} %param.5, f32[]{:T(128)S(6)} %div.21, bf16[4,416,3328]{2,1,0:T(8,128)(2,1)} %all-to-all-done.3, f32[3328,1664]{0,1:T(8,128)} %copy.18, s32[16,13312]{1,0:T(8,128)} %param.9, s32[]{:T(128)S(6)} %select_n.7, s32[]{:T(128)S(6)} %select_n.6), kind=kOutput, calls=%fused_computation.7 | convolution fusion | flops 254818304 | bytes 55697428 | tf_op jit(solution)/shard_map/sa,sb->ab/dot_general | solution.py:79
  848.6 40.2 %all-reduce.1 = (f32[]{:T(128)}, f32[]{:T(128)}) all-reduce(f32[]{:T(128)} %get-tuple-element.4, f32[]{:T(128)} %get-tuple-element.3), channel_id=1, replica_groups=mesh['up'=8,'dn'=4] {'up','dn'}, use_global_device_ids=true, to_apply=%region_5.0 | all-reduce | flops 2 | bytes 16 | tf_op jit(solution)/shard_map/psum | solution.py:106
  892.3 29.5 %fusion.13 = (bf16[1664,3328]{1,0:T(8,128)(2,1)}, f32[1664,3328]{1,0:T(8,128)}) fusion(f32[]{:T(128)} %sqrt.10, f32[]{:T(128)} %get-tuple-element.10, bf16[1664,3328]{1,0:T(8,128)(2,1)} %param.5, bf16[1664,3328]{1,0:T(8,128)(2,1)} %get-tuple-element.14, f32[]{:T(128)S(6)} %div.21, bf16[4,416,3328]{2,1,0:T(8,128)(2,1)} %all-to-all-done.3, f32[3328,1664]{0,1:T(8,128)} %copy.18), kind=kLoop, calls=%fused_computation.31 | loop fusion | flops 66453504 | bytes 88604688 | tf_op jit(solution)/shard_map/convert_element_type | solution.py:90
  921.8 16.3 copy.19
  938.2 128.9 %all_to_all.41.x_ref = bf16[8,416,1664]{2,1,0:T(8,128)(2,1)} all-to-all(bf16[8,416,1664]{2,1,0:T(8,128)(2,1)} %bitcast.54), channel_id=1, replica_groups=mesh['up'=8,'dn'=4] {'up'}, dimensions={0} | all-to-all | bytes 22151168 | tf_op jit(solution)/shard_map/all_to_all | solution.py:94
  1067.1 6.2 all-to-all-start.6
  1073.3 38.7 %shard_map.78 = bf16[8,416,1664]{2,1,0:T(8,128)(2,1)} custom-call(s32[520]{0:T(1024)} %reshape.37.columns_ref, bf16[8,416,1664]{2,1,0:T(8,128)(2,1)} %all_to_all.41.x_ref, bf16[104,640,128]{2,1,0:T(8,128)(2,1)} %bitcast.47), custom_call_target="tpu_custom_call" | custom-call | flops 7088373760 | bytes 39190528 | tf_op jit(solution)/shard_map/pallas_call | solution.py:43
  1112.0 202.3 %all-to-all-done.6.x_ref = bf16[4,416,3328]{2,1,0:T(8,128)(2,1)} async-done(((bf16[4,416,3328]{2,1,0:T(8,128)(2,1)}), bf16[4,416,3328]{2,1,0:T(8,128)(2,1)}, u32[]{:S(2)}, u32[]{:S(2)}) %all-to-all-start.6) | async-done | bytes 11075616 | tf_op jit(solution)/shard_map/all_to_all | solution.py:93
  1314.3 5.2 all-to-all-start.5
  1319.6 39.0 %shard_map.79 = bf16[4,416,3328]{2,1,0:T(8,128)(2,1)} custom-call(s32[520]{0:T(1024)} %reshape.37.columns_ref, bf16[4,416,3328]{2,1,0:T(8,128)(2,1)} %all-to-all-done.6.x_ref, bf16[104,640,128]{2,1,0:T(8,128)(2,1)} %bitcast.48), custom_call_target="tpu_custom_call" | custom-call | flops 7088373760 | bytes 39190528 | tf_op jit(solution)/shard_map/pallas_call | solution.py:43
  1358.5 83.9 %all-to-all-done.5 = bf16[8,416,1664]{2,1,0:T(8,128)(2,1)} async-done(((bf16[8,416,1664]{2,1,0:T(8,128)(2,1)}), bf16[8,416,1664]{2,1,0:T(8,128)(2,1)}, u32[]{:S(2)}, u32[]{:S(2)}) %all-to-all-start.5) | async-done | bytes 11075616 | tf_op jit(solution)/shard_map/all_to_all | solution.py:98
  1442.4 6.1 all-to-all-start.7
  1448.5 12.2 bitcast_convert_fusion
  1460.7 22.8 %copy.20 = f32[3328,1664]{0,1:T(8,128)} copy(f32[3328,1664]{1,0:T(8,128)} %bitcast_convert_fusion) | data formatting | bytes 44302336 | tf_op jit(solution)/shard_map/convert_element_type | solution.py:101
  1483.5 202.9 %all-to-all-done.7 = bf16[4,416,3328]{2,1,0:T(8,128)(2,1)} async-done(((bf16[4,416,3328]{2,1,0:T(8,128)(2,1)}), bf16[4,416,3328]{2,1,0:T(8,128)(2,1)}, u32[]{:S(2)}, u32[]{:S(2)}) %all-to-all-start.7) | async-done | bytes 11075616 | tf_op jit(solution)/shard_map/all_to_all | solution.py:96
  1686.4 34.1 %multiply_reduce_fusion.1 = (f32[]{:T(128)}, f32[]{:T(128)}, f32[1664,3328]{1,0:T(8,128)}) fusion(f32[1664,3328]{1,0:T(8,128)} %get-tuple-element.13, f32[]{:T(128)S(6)} %div.21, bf16[1664,3328]{1,0:T(8,128)(2,1)} %param.5, f32[]{:T(128)} %sqrt.10, bf16[1664,3328]{1,0:T(8,128)(2,1)} %get-tuple-element.14, bf16[4,416,3328]{2,1,0:T(8,128)(2,1)} %all-to-all-done.7, ...), kind=kLoop, calls=%fused_computation.19 | loop fusion | flops 71991296 | bytes 99680272 | tf_op jit(solution)/shard_map/reduce_sum | solution.py:106
  1720.5 39.2 %all-reduce = (f32[]{:T(128)}, f32[]{:T(128)}) all-reduce(f32[]{:T(128)} %get-tuple-element.6, f32[]{:T(128)} %get-tuple-element.5), channel_id=1, replica_groups=mesh['up'=8,'dn'=4] {'up','dn'}, use_global_device_ids=true, to_apply=%region_9.0 | all-reduce | flops 2 | bytes 16 | tf_op jit(solution)/shard_map/psum | solution.py:106
  1763.1 19.5 %divide_convert_fusion = bf16[1664,3328]{1,0:T(8,128)(2,1)} fusion(f32[1664,3328]{1,0:T(8,128)} %get-tuple-element.11, f32[1664,3328]{1,0:T(8,128)} %get-tuple-element.13, f32[]{:T(128)} %sqrt.11, f32[]{:T(128)} %get-tuple-element.8), kind=kLoop, calls=%fused_computation.17 | loop fusion | flops 22151168 | bytes 55377928 | tf_op jit(solution)/shard_map/convert_element_type | solution.py:115
  1782.6 1.9 pad_maximum_fusion
  (1 shorter events, 0.0 us)
Async XLA Ops:
  17.8 135.9 %copy-start.1 = (s32[104,5]{0,1:T(8,128)S(1)}, s32[104,5]{0,1:T(8,128)}, u32[]{:S(2)}) copy-start(s32[104,5]{0,1:T(8,128)} %param.8) | copy-start | bytes 6244
  17.9 136.1 %copy-start = (s32[104,5]{0,1:T(8,128)S(1)}, s32[104,5]{0,1:T(8,128)}, u32[]{:S(2)}) copy-start(s32[104,5]{0,1:T(8,128)} %param.7) | copy-start | bytes 6244
  147.6 247.6 %all-to-all-start.2 = ((bf16[4,416,3328]{2,1,0:T(8,128)(2,1)}), bf16[4,416,3328]{2,1,0:T(8,128)(2,1)}, u32[]{:S(2)}, u32[]{:S(2)}) async-start(bf16[4,416,3328]{2,1,0:T(8,128)(2,1)} %bitcast.50), calls=%async_computation.2 | async-start | bytes 22151168 | tf_op jit(solution)/shard_map/all_to_all | solution.py:93
  395.3 128.0 %all-to-all-start.1 = ((bf16[8,416,1664]{2,1,0:T(8,128)(2,1)}), bf16[8,416,1664]{2,1,0:T(8,128)(2,1)}, u32[]{:S(2)}, u32[]{:S(2)}) async-start(bf16[8,416,1664]{2,1,0:T(8,128)(2,1)} %shard_map.76), calls=%async_computation.1 | async-start | bytes 22151168 | tf_op jit(solution)/shard_map/all_to_all | solution.py:98
  523.3 302.4 %all-to-all-start.3 = ((bf16[4,416,3328]{2,1,0:T(8,128)(2,1)}), bf16[4,416,3328]{2,1,0:T(8,128)(2,1)}, u32[]{:S(2)}, u32[]{:S(2)}) async-start(bf16[4,416,3328]{2,1,0:T(8,128)(2,1)} %shard_map.77), calls=%async_computation.3 | async-start | bytes 22151168 | tf_op jit(solution)/shard_map/all_to_all | solution.py:96
  1067.1 247.2 %all-to-all-start.6 = ((bf16[4,416,3328]{2,1,0:T(8,128)(2,1)}), bf16[4,416,3328]{2,1,0:T(8,128)(2,1)}, u32[]{:S(2)}, u32[]{:S(2)}) async-start(bf16[4,416,3328]{2,1,0:T(8,128)(2,1)} %bitcast.52), calls=%async_computation.6 | async-start | bytes 22151168 | tf_op jit(solution)/shard_map/all_to_all | solution.py:93
  1314.3 128.0 %all-to-all-start.5 = ((bf16[8,416,1664]{2,1,0:T(8,128)(2,1)}), bf16[8,416,1664]{2,1,0:T(8,128)(2,1)}, u32[]{:S(2)}, u32[]{:S(2)}) async-start(bf16[8,416,1664]{2,1,0:T(8,128)(2,1)} %shard_map.78), calls=%async_computation.5 | async-start | bytes 22151168 | tf_op jit(solution)/shard_map/all_to_all | solution.py:98
  1442.4 244.1 %all-to-all-start.7 = ((bf16[4,416,3328]{2,1,0:T(8,128)(2,1)}), bf16[4,416,3328]{2,1,0:T(8,128)(2,1)}, u32[]{:S(2)}, u32[]{:S(2)}) async-start(bf16[4,416,3328]{2,1,0:T(8,128)(2,1)} %shard_map.79), calls=%async_computation.7 | async-start | bytes 22151168 | tf_op jit(solution)/shard_map/all_to_all | solution.py:96
where the time goes:
time: 1790 us; the launch traced here: 1780 us
  waiting for transfers between devices  738 us (41%)
  blocking collectives  587 us (33%)
  Pallas kernels  155 us (9%)
  other arithmetic  134 us (7%)
  local copies, waits for them, and re-layouts  103 us (6%)
  starting transfers between devices  34.8 us (2%)
  matrix products  22.9 us (1%)
    all_to_all x4, waiting for transfers between devices, body(): down = lax.all_to_all(down, 'dn', 0, 0, tiled=True)  570 us
    all_to_all x2, blocking collectives, body(): up = lax.all_to_all(up, 'up', 0, 0, tiled=True)  259 us
    psum x1, blocking collectives, body(): lax.psum(jnp.sum(jnp.square(start_vector.astype(jnp.float32))), ('up', 'd...  249 us
    all_to_all x2, waiting for transfers between devices, body(): up = lax.all_to_all(up, 'up', 0, 0, tiled=True)  168 us
    pallas_call x4, Pallas kernels, hop_blocks(): pl.pallas_call(functools.partial(hop_kernel, tile_k, tile, group, parts_t...  155 us
    psum x2, blocking collectives, body(): lax.psum((jnp.sum(work * vector), jnp.sum(work * work)), ('up', 'dn'))  79.4 us
    convert_element_type x2, local copies, waits for them, and re-layouts, body(): hopped = hopped_up.astype(jnp.float32) + hopped_down.astype(jnp.float32)  45.6 us
  transfers between devices with their start and end apart: 6, of which 5 were waited for; matrix products, arithmetic and copies ran while one was open for 7% of the time, Pallas kernels for 9%

commit v1 on v0

--- a/solution.py
+++ b/solution.py
@@ -116,8 +116,593 @@
     return (final, jnp.stack(alpha_list), jnp.stack(beta_list))
 
 
+MESH = pl.DeviceIdType.MESH
+ANY = pl.ANY
+
+
+def remote(src, dst, send_sem, recv_sem, axis, peer):
+    return pltpu.make_async_remote_copy(
+        src_ref=src,
+        dst_ref=dst,
+        send_sem=send_sem,
+        recv_sem=recv_sem,
+        device_id={axis: peer},
+        device_id_type=MESH,
+    )
+
+
+def reduce_all(n_up, n_dn, me_up, me_dn, mine, z_slots, up_slots, sems):
+    z_send, z_recv, up_send, up_recv = sems
+    z_slots[me_dn] = mine[...]
+    copies = []
+    for d in range(1, n_dn):
+        peer = lax.rem(me_dn + d, n_dn)
+        copy = remote(mine, z_slots.at[me_dn], z_send.at[d - 1], z_recv.at[me_dn], "dn", peer)
+        copy.start()
+        copies.append(copy)
+    for d in range(1, n_dn):
+        peer = lax.rem(me_dn + d, n_dn)
+        remote(mine, z_slots.at[peer], z_send.at[d - 1], z_recv.at[peer], "dn", peer).wait_recv()
+    for copy in copies:
+        copy.wait_send()
+    mine[...] = jnp.sum(z_slots[...], axis=0)
+    up_slots[me_up] = mine[...]
+    copies = []
+    for d in range(1, n_up):
+        peer = lax.rem(me_up + d, n_up)
+        copy = remote(mine, up_slots.at[me_up], up_send.at[d - 1], up_recv.at[me_up], "up", peer)
+        copy.start()
+        copies.append(copy)
+    for d in range(1, n_up):
+        peer = lax.rem(me_up + d, n_up)
+        remote(mine, up_slots.at[peer], up_send.at[d - 1], up_recv.at[peer], "up", peer).wait_recv()
+    for copy in copies:
+        copy.wait_send()
+    return jnp.sum(up_slots[...], axis=0)
+
+
+def fold(x):
+    return jnp.sum(x.reshape(-1, 8, x.shape[-1]), axis=0)
+
+
+def kernel(
+    dims, columns, signs, v, tiles, occ_all, occ_mine, rows_t, cols_t,
+    m_out, w_out, sigma_out, gram_out,
+    d0, s0, u0, r0, x1, x2, dn1, s1, u2, g2, d2, vt, dt, r2,
+    x, y, w, a, b, staged, flat, turned, made, first, last, z_first, up_first, z_last, up_last,
+    local, stage_sem, strip_sem, made_sem, a_send, a_recv, b_send, b_recv, c_send, c_recv,
+    p_send, p_recv, q_send, q_recv, t_send, t_recv, o_send, o_recv, first_sems, last_sems,
+):
+    n_up, n_dn, count, tile_k, tile, group, spans = dims
+    rows, cols = v.shape
+    half = cols // 2
+    wide_tiles = cols // tile
+    tall_tiles = rows // tile
+    half_tiles = wide_tiles // 2
+    piece = x.shape[1]
+    me_up = lax.axis_index("up")
+    me_dn = lax.axis_index("dn")
+
+    barrier = pltpu.get_barrier_semaphore()
+    for d in range(1, n_dn):
+        pl.semaphore_signal(
+            barrier, inc=1, device_id={"dn": lax.rem(me_dn + d, n_dn)}, device_id_type=MESH
+        )
+    for d in range(1, n_up):
+        pl.semaphore_signal(
+            barrier, inc=1, device_id={"up": lax.rem(me_up + d, n_up)}, device_id_type=MESH
+        )
+    pl.semaphore_wait(barrier, n_dn + n_up - 2)
+
+    def lanes(start, size):
+        return pl.ds(pl.multiple_of(start, tile), size)
+
+    def subs(start, size):
+        return pl.ds(pl.multiple_of(start, 8), size)
+
+    def peers(axis):
+        n, me = (n_dn, me_dn) if axis == "dn" else (n_up, me_up)
+        return [lax.rem(me + d, n) for d in range(1, n)]
+
+    started = []
+
+    def launch(copies):
+        for copy in copies:
+            copy.start()
+        started.extend(copies)
+
+    def arrive(copies):
+        for copy in copies:
+            copy.wait_recv()
+
+    def z_in(c, receiving):
+        return [
+            remote(
+                v.at[subs(peer * 2 * piece + c * piece, piece), :],
+                x1.at[c, :, lanes((peer if receiving else me_dn) * cols, cols)],
+                a_send.at[c, k], a_recv.at[c, peer if receiving else me_dn], "dn", peer,
+            )
+            for k, peer in enumerate(peers("dn"))
+        ]
+
+    def z_out(source, target, send, recv, span, slot, c, receiving):
+        low, high = span
+        return [
+            remote(
+                source.at[c, pl.ds(peer * wide_tiles + low, high - low)],
+                target.at[
+                    pl.ds(low, high - low),
+                    subs((peer if receiving else me_dn) * 2 * piece + c * piece, piece),
+                    :,
+                ],
+                send.at[2 * slot + c, k],
+                recv.at[2 * slot + c, peer if receiving else me_dn],
+                "dn", peer,
+            )
+            for k, peer in enumerate(peers("dn"))
+        ]
+
+    halves = ((0, half_tiles), (half_tiles, wide_tiles))
+
+    def up_in(source, target, send, recv, h, receiving):
+        return [
+            remote(
+                source.at[:, subs(h * half + peer * piece, piece), :],
+                target.at[h, pl.ds((peer if receiving else me_up) * tall_tiles, tall_tiles)],
+                send.at[h, k], recv.at[h, peer if receiving else me_up], "up", peer,
+            )
+            for k, peer in enumerate(peers("up"))
+        ]
+
+    def up_out(source, target, send, recv, h, receiving):
+        return [
+            remote(
+                source.at[h, pl.ds(peer * tall_tiles, tall_tiles)],
+                target.at[:, subs(h * half + (peer if receiving else me_up) * piece, piece), :],
+                send.at[h, k], recv.at[h, peer if receiving else me_up], "up", peer,
+            )
+            for k, peer in enumerate(peers("up"))
+        ]
+
+    def hop():
+        def one(i, carry):
+            picked = [x[columns[i * tile_k + k]] for k in range(tile_k)]
+            result = jnp.dot(
+                jnp.concatenate(picked, axis=1), w[i], preferred_element_type=jnp.float32
+            )
+            y[i] = result.astype(jnp.bfloat16)
+            return carry
+
+        lax.fori_loop(0, count, one, 0, unroll=2)
+
+    def run(copies):
+        for copy in copies:
+            copy.start()
+        finish(copies)
+
+    def finish(copies):
+        for copy in copies:
+            copy.wait()
+
+    def load_rows(c):
+        for k, peer in enumerate(peers("dn") + [me_dn]):
+            start = me_dn * 2 * piece + c * piece
+
+            def one(t, carry):
+                at = lanes(t * tile, tile)
+                wide = lanes((peer * wide_tiles + t) * tile, tile)
+                source = v.at[subs(start, piece), at] if k == n_dn - 1 else x1.at[c, :, wide]
+                pltpu.make_async_copy(source, x.at[peer * wide_tiles + t], local.at[k]).start()
+                return carry
+
+            lax.fori_loop(0, wide_tiles, one, 0)
+        for k, peer in enumerate(peers("dn") + [me_dn]):
+            block = x.at[pl.ds(peer * wide_tiles, wide_tiles)]
+            pltpu.make_async_copy(block, block, local.at[k]).wait()
+
+    def load_columns(target, source, h):
+        copies = []
+        for k, peer in enumerate(peers("up")):
+            at = pl.ds(peer * tall_tiles, tall_tiles)
+            copies.append(pltpu.make_async_copy(target.at[h, at], x.at[at], local.at[k]))
+        copies.append(
+            pltpu.make_async_copy(
+                source.at[:, subs(h * half + me_up * piece, piece), :],
+                x.at[pl.ds(me_up * tall_tiles, tall_tiles)],
+                local.at[n_up - 1],
+            )
+        )
+        run(copies)
+
+    def keep_rows(target, own_target, c):
+        copies = [
+            pltpu.make_async_copy(y, target.at[c], local.at[0]),
+            pltpu.make_async_copy(
+                y.at[pl.ds(me_dn * wide_tiles, wide_tiles)],
+                own_target.at[:, subs(me_dn * 2 * piece + c * piece, piece), :],
+                local.at[1],
+            ),
+        ]
+        for copy in copies:
+            copy.start()
+        return copies
+
+    def keep_columns(target, own_target, h):
+        copies = [
+            pltpu.make_async_copy(y, target.at[h], local.at[0]),
+            pltpu.make_async_copy(
+                y.at[pl.ds(me_up * tall_tiles, tall_tiles)],
+                own_target.at[:, subs(h * half + me_up * piece, piece), :],
+                local.at[1],
+            ),
+        ]
+        for copy in copies:
+            copy.start()
+        return copies
+
+    def turn(target, h, each):
+        def one(i, carry):
+            strip = a[i]
+            flipped = strip.T
+            for j in range(tall_tiles):
+                b[j, subs(i * tile, tile), :] = flipped[:, j * tile : (j + 1) * tile]
+            return each(i, strip, carry)
+
+        carry = lax.fori_loop(0, half_tiles, one, each(None, None, None))
+        run([pltpu.make_async_copy(b, target.at[:, subs(h * half, half), :], local.at[0])])
+        return carry
+
+    for c in range(2):
+        launch(z_in(c, False))
+
+    def moments(h):
+        def each(i, strip, carry):
+            if i is None:
+                return (jnp.zeros((8, tile), jnp.float32), jnp.zeros((8, tile), jnp.float32))
+            diagonal = jnp.dot(
+                rows_t[...], occ_mine[:, lanes(h * half + i * tile, tile)],
+                preferred_element_type=jnp.float32,
+            )
+            value = strip.astype(jnp.float32)
+            square = value * value
+            return (carry[0] + fold(diagonal * square), carry[1] + fold(square))
+
+        return each
+
+    def nothing(i, strip, carry):
+        return 0
+
+    sums = []
+    for h in range(2):
+
+        def fetch(i, carry):
+            pltpu.make_async_copy(
+                v.at[:, lanes(h * half + i * tile, tile)], a.at[i], local.at[0]
+            ).start()
+            return carry
+
+        lax.fori_loop(0, half_tiles, fetch, 0)
+        pltpu.make_async_copy(a, a, local.at[0]).wait()
+        sums.append(turn(vt, h, moments(h)))
+        launch(up_in(vt, x2, p_send, p_recv, h, False))
+    weighted = jnp.sum(sums[0][0] + sums[1][0], axis=0, keepdims=True)
+    norm = jnp.sum(sums[0][1] + sums[1][1], axis=0, keepdims=True)
+    row = lax.broadcasted_iota(jnp.int32, (8, tile), 0)
+    first[...] = jnp.where(row == 0, weighted, jnp.where(row == 1, norm, 0.0))
+
+    def stage(g, slot):
+        return pltpu.make_async_copy(
+            tiles.at[pl.ds(g * group, group)], staged.at[slot], stage_sem.at[slot]
+        )
+
+    stage(0, 0).start()
+
+    def prepare(g, carry):
+        slot = lax.rem(g, 2)
+
+        @pl.when(g + 1 < count // group)
+        def _():
+            stage(g + 1, 1 - slot).start()
+
+        stage(g, slot).wait()
+
+        def one(t, inner):
+            for k in range(tile_k):
+                i = g * group + t
+                sign = (1 - 2 * signs[i * tile_k + k]).astype(jnp.float32)
+                value = staged[slot, t, k].astype(jnp.float32) * sign
+                w[i, k * tile : (k + 1) * tile, :] = value.astype(jnp.bfloat16).T
+            return inner
+
+        return lax.fori_loop(0, group, one, carry)
+
+    lax.fori_loop(0, count // group, prepare, 0)
+
+    totals = reduce_all(n_up, n_dn, me_up, me_dn, first, z_first, up_first, first_sems)
+    sigma = coupling * jnp.sum(totals[0:1, :]) / jnp.maximum(jnp.sum(totals[1:2, :]), 1e-30)
+    sigma_out[...] = jnp.full((8, tile), sigma, jnp.float32)
+
+    def shifted(left, store):
+        def one(j, carry):
+            diagonal = coupling * jnp.dot(
+                left, occ_all[:, lanes(j * tile, tile)], preferred_element_type=jnp.float32
+            )
+            value = y[j].astype(jnp.float32) + (diagonal - sigma) * x[j].astype(jnp.float32)
+            store[j] = value.astype(jnp.bfloat16)
+            return carry
+
+        lax.fori_loop(0, count, one, 0, unroll=2)
+
+    for h in range(2):
+        arrive(up_in(vt, x2, p_send, p_recv, h, True))
+        load_columns(x2, vt, h)
+        hop()
+        finish(keep_columns(u2, u0, h))
+        launch(up_out(u2, u0, q_send, q_recv, h, False))
+        shifted(cols_t[subs(h * half + me_up * piece, piece), :], y)
+        run([pltpu.make_async_copy(y, g2.at[h], local.at[0])])
+
+    for c in range(2):
+        arrive(z_in(c, True))
+        load_rows(c)
+        hop()
+        finish(keep_rows(dn1, d0, c))
+        if c == 0:
+            launch(z_out(dn1, d0, b_send, b_recv, halves[0], 0, 0, False))
+        else:
+            launch(z_out(dn1, d0, b_send, b_recv, halves[0], 0, 1, False))
+            launch(z_out(dn1, d0, b_send, b_recv, halves[1], 1, 0, False))
+            launch(z_out(dn1, d0, b_send, b_recv, halves[1], 1, 1, False))
+        shifted(rows_t[subs(me_dn * 2 * piece + c * piece, piece), :], x)
+        hop()
+        finish(keep_rows(s1, s0, c))
+
+    def flip(h):
+        for c in range(2):
+            arrive(z_out(dn1, d0, b_send, b_recv, halves[h], h, c, True))
+        run([pltpu.make_async_copy(d0.at[pl.ds(h * half_tiles, half_tiles)], a, local.at[0])])
+        turn(dt, h, nothing)
+        launch(up_in(dt, d2, t_send, t_recv, h, False))
+
+    def second(h):
+        arrive(up_in(dt, d2, t_send, t_recv, h, True))
+        load_columns(d2, dt, h)
+        run([pltpu.make_async_copy(g2.at[h], y, local.at[0])])
+
+        def one(j, carry):
+            value = y[j].astype(jnp.float32) + 2.0 * x[j].astype(jnp.float32)
+            x[j] = value.astype(jnp.bfloat16)
+            return carry
+
+        lax.fori_loop(0, count, one, 0, unroll=2)
+        hop()
+        finish(keep_columns(r2, r0, h))
+        launch(up_out(r2, r0, o_send, o_recv, h, False))
+
+    flip(0)
+    for slot, span in enumerate(spans):
+        for c in range(2):
+            launch(z_out(s1, s0, c_send, c_recv, span, slot, c, False))
+    second(0)
+    flip(1)
+    second(1)
+
+    def strip_in(i, slot):
+        at = subs(i * tile, tile)
+        return [
+            pltpu.make_async_copy(v.at[:, lanes(i * tile, tile)], flat.at[slot, 0], strip_sem.at[slot, 0]),
+            pltpu.make_async_copy(d0.at[i], flat.at[slot, 1], strip_sem.at[slot, 1]),
+            pltpu.make_async_copy(s0.at[i], flat.at[slot, 2], strip_sem.at[slot, 2]),
+            pltpu.make_async_copy(u0.at[:, at, :], turned.at[slot, 0], strip_sem.at[slot, 3]),
+            pltpu.make_async_copy(r0.at[:, at, :], turned.at[slot, 1], strip_sem.at[slot, 4]),
+        ]
+
+    def strip_out(i, slot):
+        return [
+            pltpu.make_async_copy(made.at[slot, 0], m_out.at[i], made_sem.at[slot, 0]),
+            pltpu.make_async_copy(made.at[slot, 1], w_out.at[i], made_sem.at[slot, 1]),
+        ]
+
+    def combine(low, high, carry):
+        for copy in strip_in(low, 0):
+            copy.start()
+
+        def one(i, carry):
+            slot = lax.rem(i - low, 2)
+
+            @pl.when(i + 1 < high)
+            def _():
+                for copy in strip_in(i + 1, 1 - slot):
+                    copy.start()
+
+            finish(strip_in(i, slot))
+
+            @pl.when(i - low >= 2)
+            def _():
+                finish(strip_out(i - 2, slot))
+
+            def block(j, carry):
+                at = subs(j * tile, tile)
+                value = flat[slot, 0, at, :].astype(jnp.float32)
+                diagonal = coupling * jnp.dot(
+                    rows_t[at, :], occ_mine[:, lanes(i * tile, tile)],
+                    preferred_element_type=jnp.float32,
+                )
+                shift = diagonal - sigma
+                total = flat[slot, 1, at, :].astype(jnp.float32)
+                total = total + turned[slot, 0, j].T.astype(jnp.float32) + shift * value
+                m = flat[slot, 2, at, :].astype(jnp.float32)
+                m = m + turned[slot, 1, j].T.astype(jnp.float32) + shift * total
+                made[slot, 0, at, :] = m.astype(jnp.bfloat16)
+                made[slot, 1, at, :] = total.astype(jnp.bfloat16)
+                pairs = (m * m, m * total, m * value, total * total, total * value, value * value)
+                return tuple(c + fold(p) for c, p in zip(carry, pairs))
+
+            carry = lax.fori_loop(0, tall_tiles, block, carry)
+            for copy in strip_out(i, slot):
+                copy.start()
+            return carry
+
+        carry = lax.fori_loop(low, high, one, carry)
+        for i in range(max(low, high - 2), high):
+            finish(strip_out(i, (i - low) % 2))
+        return carry
+
+    carry = tuple(jnp.zeros((8, tile), jnp.float32) for _ in range(6))
+    for h in range(2):
+        arrive(up_out(u2, u0, q_send, q_recv, h, True))
+        arrive(up_out(r2, r0, o_send, o_recv, h, True))
+    for slot, span in enumerate(spans):
+        for c in range(2):
+            arrive(z_out(s1, s0, c_send, c_recv, span, slot, c, True))
+        carry = combine(span[0], span[1], carry)
+    packed = jnp.zeros((8, tile), jnp.float32)
+    for k in range(6):
+        packed = jnp.where(row == k, jnp.sum(carry[k], axis=0, keepdims=True), packed)
+    last[...] = packed
+    gram_out[...] = reduce_all(n_up, n_dn, me_up, me_dn, last, z_last, up_last, last_sems)
+    for copy in started:
+        copy.wait_send()
+
+
+def exchange(v, tiles, columns, signs, occ_all, occ_mine, rows_t, cols_t):
+    n_up = lax.axis_size("up")
+    n_dn = lax.axis_size("dn")
+    count, tile_k, tile, _ = tiles.shape
+    rows, cols = v.shape
+    piece = rows // n_dn // 2
+    group = max(d for d in range(1, 9) if count % d == 0)
+    wide, tall = cols // tile, rows // tile
+    cuts = sorted({0, wide // 2, wide - wide // 4, wide - wide // 12, wide})
+    spans = tuple(zip(cuts[:-1], cuts[1:]))
+    bf16, f32 = jnp.bfloat16, jnp.float32
+    natural = jax.ShapeDtypeStruct((wide, rows, tile), bf16)
+    turned = jax.ShapeDtypeStruct((tall, cols, tile), bf16)
+    strips = jax.ShapeDtypeStruct((2, count, piece, tile), bf16)
+    landed = jax.ShapeDtypeStruct((2, piece, count * tile), bf16)
+    small = jax.ShapeDtypeStruct((8, tile), f32)
+    dma = pltpu.SemaphoreType.DMA
+    z4 = [dma((4, n_dn - 1)), dma((4, n_dn))]
+    zs = [dma((2 * len(spans), n_dn - 1)), dma((2 * len(spans), n_dn))]
+    up2 = [dma((2, n_up - 1)), dma((2, n_up))]
+    sums = [dma((n_dn - 1,)), dma((n_dn,)), dma((n_up - 1,)), dma((n_up,))]
+    any_spec = pl.BlockSpec(memory_space=ANY)
+    vmem = pl.BlockSpec(memory_space=pltpu.VMEM)
+    smem = pl.BlockSpec(memory_space=pltpu.SMEM)
+    outs = pl.pallas_call(
+        functools.partial(kernel, (n_up, n_dn, count, tile_k, tile, group, spans)),
+        in_specs=[smem, smem, any_spec, any_spec, vmem, vmem, vmem, vmem],
+        out_specs=[any_spec] * 2 + [vmem] * 2 + [any_spec] * 14,
+        out_shape=[natural, natural, small, small, natural, natural, turned, turned, landed]
+        + [strips] * 6 + [turned, turned, strips],
+        scratch_shapes=[
+            pltpu.VMEM((count, piece, tile), bf16),
+            pltpu.VMEM((count, piece, tile), bf16),
+            pltpu.VMEM((count, tile_k * tile, tile), bf16),
+            pltpu.VMEM((wide // 2, rows, tile), bf16),
+            pltpu.VMEM((tall, cols // 2, tile), bf16),
+            pltpu.VMEM((2, group, tile_k, tile, tile), bf16),
+            pltpu.VMEM((2, 3, rows, tile), bf16),
+            pltpu.VMEM((2, 2, tall, tile, tile), bf16),
+            pltpu.VMEM((2, 2, rows, tile), bf16),
+            pltpu.VMEM((8, tile), f32),
+            pltpu.VMEM((8, tile), f32),
+            pltpu.VMEM((n_dn, 8, tile), f32),
+            pltpu.VMEM((n_up, 8, tile), f32),
+            pltpu.VMEM((n_dn, 8, tile), f32),
+            pltpu.VMEM((n_up, 8, tile), f32),
+            dma((max(n_up, n_dn),)),
+            dma((2,)),
+            dma((2, 5)),
+            dma((2, 2)),
+            dma((2, n_dn - 1)), dma((2, n_dn)),
+            *z4, *zs, *up2, *up2, *up2, *up2, sums, sums,
+        ],
+        compiler_params=pltpu.CompilerParams(
+            collective_id=0, has_side_effects=True, vmem_limit_bytes=60 * 1024 * 1024
+        ),
+        cost_estimate=pl.CostEstimate(
+            flops=8 * rows * cols * tile_k * tile, bytes_accessed=60 * rows * cols, transcendentals=0
+        ),
+    )(columns, signs, v, tiles, occ_all, occ_mine, rows_t, cols_t)
+    return outs[:4]
+
+
+def final_kernel(m, w, v, sigma, gram, out, scalars):
+    mm, mw, mv, ww, wv, vv = (jnp.sum(gram[k : k + 1, :], axis=1, keepdims=True) for k in range(6))
+    shift = sigma[0:1, 0:1]
+    scale = 1.0 / jnp.maximum(jnp.sqrt(vv), 1.0)
+    square = scale * scale
+    alpha1 = square * (wv + shift * vv)
+    delta = alpha1 - shift
+    norm = ww - 2.0 * delta * wv + delta * delta * vv
+    beta1 = jnp.sqrt(jnp.maximum(square * norm, 1.0))
+    gain = square / (beta1 * beta1)
+    length = gain * norm
+    offset = mw - delta * mv - delta * (ww - delta * wv) - beta1 * beta1 * (wv - delta * vv)
+    offset = gain * offset
+    alpha2 = offset + shift * length
+    c1 = -(delta + offset + shift * (length - 1.0))
+    c2 = (alpha2 - shift) * delta - beta1 * beta1
+    residual = mm + c1 * c1 * ww + c2 * c2 * vv + 2.0 * (c1 * mw + c2 * mv + c1 * c2 * wv)
+    beta2 = jnp.sqrt(jnp.maximum(gain * residual, 1.0))
+    factor = scale / (beta1 * beta2)
+    value = m[0].astype(jnp.float32) + c1 * w[0].astype(jnp.float32) + c2 * v[...].astype(jnp.float32)
+    out[...] = (factor * value).astype(jnp.bfloat16)
+    row = lax.broadcasted_iota(jnp.int32, scalars.shape, 0)
+    found = jnp.zeros(scalars.shape, jnp.float32)
+    for k, value in enumerate((alpha1, alpha2, beta1, beta2)):
+        found = jnp.where(row == k, value, found)
+    scalars[...] = found
+
+
+def finish_all(m, w, v, sigma, gram):
+    rows, cols = v.shape
+    tile = m.shape[2]
+    column = pl.BlockSpec((rows, tile), lambda i: (0, i))
+    strip = pl.BlockSpec((1, rows, tile), lambda i: (i, 0, 0))
+    small = pl.BlockSpec((8, tile), lambda i: (0, 0))
+    return pl.pallas_call(
+        final_kernel,
+        grid=(cols // tile,),
+        in_specs=[strip, strip, column, small, small],
+        out_specs=[column, small],
+        out_shape=[
+            jax.ShapeDtypeStruct((rows, cols), jnp.bfloat16),
+            jax.ShapeDtypeStruct((8, tile), jnp.float32),
+        ],
+    )(m, w, v, sigma, gram)
+
+
+def fused_body(start_vector, hop_tiles, tile_columns, tile_signs, occupation):
+    rows, cols = start_vector.shape
+    row_start = lax.axis_index("up") * rows
+    col_start = lax.axis_index("dn") * cols
+    occ = occupation.astype(jnp.bfloat16)
+    occ_mine = lax.dynamic_slice_in_dim(occ, col_start, cols, 1)
+    rows_t = lax.dynamic_slice_in_dim(occ, row_start, rows, 1).T
+    cols_t = occ_mine.T
+    m, w, sigma, gram = exchange(
+        start_vector, hop_tiles, tile_columns.reshape(-1), tile_signs.reshape(-1),
+        occ, occ_mine, rows_t, cols_t,
+    )
+    final, scalars = finish_all(m, w, start_vector, sigma, gram)
+    return (final, scalars[0:2, 0], scalars[2:4, 0])
+
+
+def fits(n_up, n_dn, rows, cols, tile):
+    even = rows % (16 * n_dn) == 0 and cols % (16 * n_up) == 0
+    return even and rows % tile == 0 and cols % (2 * tile) == 0
+
+
+def chosen_body(start_vector, hop_tiles, *rest):
+    rows, cols = start_vector.shape
+    good = fits(lax.axis_size("up"), lax.axis_size("dn"), rows, cols, hop_tiles.shape[2])
+    return (fused_body if good else body)(start_vector, hop_tiles, *rest)
+
+
 def solution(mesh):
     placed = (P("up", "dn"), P(), P(), P(), P())
     return jax.shard_map(
-        body, mesh=mesh, in_specs=placed, out_specs=(P("up", "dn"), P(), P()), check_vma=False
+        chosen_body, mesh=mesh, in_specs=placed, out_specs=(P("up", "dn"), P(), P()), check_vma=False
     )

time: 1790 us -> 942 us (0.53)
  Pallas kernels: 155 us -> 932 us
  waiting for transfers between devices: 738 us -> 0 us
  blocking collectives: 587 us -> 0 us
  other arithmetic: 134 us -> 1.2 us
  local copies, waits for them, and re-layouts: 103 us -> 6.77 us
  starting transfers between devices: 34.8 us -> 0 us
  matrix products: 22.9 us -> 0 us
    pallas_call x4 -> x2, Pallas kernels: 155 us -> 932 us  [the longest x1 904 us: exchange(): pl.pallas_call(functools.partial(kernel, (n_up, n_dn, count, tile_k, tile...]
    all_to_all x6 -> x0, waiting for transfers between devices: 738 us -> none  [the longest x4 570 us: body(): down = lax.all_to_all(down, 'dn', 0, 0, tiled=True)]
    psum x3 -> x0, blocking collectives: 328 us -> none  [the longest x1 249 us: body(): lax.psum(jnp.sum(jnp.square(start_vector.astype(jnp.float32))), ('up', 'd...]
    all_to_all x2 -> x0, blocking collectives: 259 us -> none  [body(): up = lax.all_to_all(up, 'up', 0, 0, tiled=True)]
    convert_element_type x5 -> x1, other arithmetic: 73.4 us -> 1.2 us  [fused_body(): occ = occupation.astype(jnp.bfloat16)]
    transpose x3 -> x0, local copies, waits for them, and re-layouts: 56.3 us -> none  [the longest x2 33.6 us: body(): up = rounded.T.reshape(count_up, block_cols // count_up, block_rows)]
    convert_element_type x3 -> x0, local copies, waits for them, and re-layouts: 45.8 us -> none  [the longest x2 45.6 us: body(): hopped = hopped_up.astype(jnp.float32) + hopped_down.astype(jnp.float32)]
    reduce_sum x2 -> x0, other arithmetic: 44.5 us -> none  [the longest x1 34.1 us: body(): jnp.sum(work * vector)]
  transfers between devices with their start and end apart: 6 -> 0, of which waited for: 5 -> 0; matrix products, arithmetic and copies ran while one was open for 7% -> 0% of each run, Pallas kernels for 9% -> 0%
where the time goes in v1:
time: 942 us; the launch traced here: 941 us
  Pallas kernels  932 us (99%)
    pallas_call x1, Pallas kernels, exchange(): pl.pallas_call(functools.partial(kernel, (n_up, n_dn, count, tile_k, tile...  904 us
    pallas_call x1, Pallas kernels, finish_all(): pl.pallas_call(final_kernel, grid=(cols // tile,), in_specs=[strip, strip...  28.4 us

profile of v1, /device:TPU:0, one launch (start us, length us, event | category | flops | bytes accessed | tf_op | source)
XLA Modules:
  0.0 940.8 jit_solution(3444791724488117707)
XLA Ops:
  0.6 0.8 copy.16
  1.4 0.8 reshape.12.columns
  2.2 0.8 copy.17
  3.0 0.8 reshape.13.signs
  3.8 1.2 convert_element_type.3.occ_all
  5.0 0.0 copy-start
  5.0 0.0 copy-start.1
  5.0 1.0 copy.22
  6.0 1.2 copy.21
  7.2 0.0 copy-done
  7.2 0.0 copy-done.1
  7.2 903.8 %shard_map.76 = (bf16[26,1664,128]{2,1,0:T(8,128)(2,1)}, bf16[26,1664,128]{2,1,0:T(8,128)(2,1)}, f32[8,128]{1,0:T(8,128)}, f32[8,128]{1,0:T(8,128)}, bf16[26,166...) custom-call(s32[520]{0:T(1024)} %reshape.12.columns, ...), custom_call_target="tpu_custom_call" | custom-call | flops 28353495040 | bytes 332267520 | tf_op jit(solution)/shard_map/pallas_call | solution.py:592
  911.0 28.4 %shard_map.77 = (bf16[1664,3328]{1,0:T(8,128)(2,1)}, f32[8,128]{1,0:T(8,128)}) custom-call(bf16[26,1664,128]{2,1,0:T(8,128)(2,1)} %get-tuple-element.9.m, bf16[26,1664,128]{2,1,0:T(8,128)(2,1)} %get-tuple-element.10.w, bf16[1664,3328]{1,0:T(8,128)(2,1)} %v.3, f32[8,128]{1,0:T(8,128)} %get-tuple-element.11.sigma, f32[8,128]{1,0:T(8,128)} %get-tuple-element.12.gram), custom_call_target="tpu_custom_call" | custom-call | tf_op jit(solution)/shard_map/pallas_call | solution.py:665
  939.4 1.4 slice_reduce_fusion
  (2 shorter events, 0.0 us)
Async XLA Ops:
  5.0 2.3 copy-start
  5.0 2.2 copy-start.1

commit v2 on v1

--- a/solution.py
+++ b/solution.py
@@ -169,9 +169,9 @@
     dims, columns, signs, v, tiles, occ_all, occ_mine, rows_t, cols_t,
     m_out, w_out, sigma_out, gram_out,
     d0, s0, u0, r0, x1, x2, dn1, s1, u2, g2, d2, vt, dt, r2,
-    x, y, w, a, b, staged, flat, turned, made, first, last, z_first, up_first, z_last, up_last,
+    x, y, w, a, b, staged, flat, turned, made, last, z_last, up_last,
     local, stage_sem, strip_sem, made_sem, a_send, a_recv, b_send, b_recv, c_send, c_recv,
-    p_send, p_recv, q_send, q_recv, t_send, t_recv, o_send, o_recv, first_sems, last_sems,
+    p_send, p_recv, q_send, q_recv, t_send, t_recv, o_send, o_recv, last_sems,
 ):
     n_up, n_dn, count, tile_k, tile, group, spans = dims
     rows, cols = v.shape
@@ -179,6 +179,7 @@
     wide_tiles = cols // tile
     tall_tiles = rows // tile
     half_tiles = wide_tiles // 2
+    wide = occ_all.shape[1]
     piece = x.shape[1]
     me_up = lax.axis_index("up")
     me_dn = lax.axis_index("dn")
@@ -211,9 +212,10 @@
             copy.start()
         started.extend(copies)
 
-    def arrive(copies):
-        for copy in copies:
-            copy.wait_recv()
+    def arrive(name, copies):
+        with jax.named_scope(name):
+            for copy in copies:
+                copy.wait_recv()
 
     def z_in(c, receiving):
         return [
@@ -273,7 +275,8 @@
             y[i] = result.astype(jnp.bfloat16)
             return carry
 
-        lax.fori_loop(0, count, one, 0, unroll=2)
+        with jax.named_scope("hop"):
+            lax.fori_loop(0, count, one, 0, unroll=8)
 
     def run(copies):
         for copy in copies:
@@ -340,39 +343,19 @@
             copy.start()
         return copies
 
-    def turn(target, h, each):
+    def turn(target, h):
         def one(i, carry):
-            strip = a[i]
-            flipped = strip.T
+            flipped = a[i].T
             for j in range(tall_tiles):
                 b[j, subs(i * tile, tile), :] = flipped[:, j * tile : (j + 1) * tile]
-            return each(i, strip, carry)
-
-        carry = lax.fori_loop(0, half_tiles, one, each(None, None, None))
+            return carry
+
+        lax.fori_loop(0, half_tiles, one, 0)
         run([pltpu.make_async_copy(b, target.at[:, subs(h * half, half), :], local.at[0])])
-        return carry
 
     for c in range(2):
         launch(z_in(c, False))
 
-    def moments(h):
-        def each(i, strip, carry):
-            if i is None:
-                return (jnp.zeros((8, tile), jnp.float32), jnp.zeros((8, tile), jnp.float32))
-            diagonal = jnp.dot(
-                rows_t[...], occ_mine[:, lanes(h * half + i * tile, tile)],
-                preferred_element_type=jnp.float32,
-            )
-            value = strip.astype(jnp.float32)
-            square = value * value
-            return (carry[0] + fold(diagonal * square), carry[1] + fold(square))
-
-        return each
-
-    def nothing(i, strip, carry):
-        return 0
-
-    sums = []
     for h in range(2):
 
         def fetch(i, carry):
@@ -383,13 +366,8 @@
 
         lax.fori_loop(0, half_tiles, fetch, 0)
         pltpu.make_async_copy(a, a, local.at[0]).wait()
-        sums.append(turn(vt, h, moments(h)))
+        turn(vt, h)
         launch(up_in(vt, x2, p_send, p_recv, h, False))
-    weighted = jnp.sum(sums[0][0] + sums[1][0], axis=0, keepdims=True)
-    norm = jnp.sum(sums[0][1] + sums[1][1], axis=0, keepdims=True)
-    row = lax.broadcasted_iota(jnp.int32, (8, tile), 0)
-    first[...] = jnp.where(row == 0, weighted, jnp.where(row == 1, norm, 0.0))
-
     def stage(g, slot):
         return pltpu.make_async_copy(
             tiles.at[pl.ds(g * group, group)], staged.at[slot], stage_sem.at[slot]
@@ -416,10 +394,11 @@
 
         return lax.fori_loop(0, group, one, carry)
 
-    lax.fori_loop(0, count // group, prepare, 0)
-
-    totals = reduce_all(n_up, n_dn, me_up, me_dn, first, z_first, up_first, first_sems)
-    sigma = coupling * jnp.sum(totals[0:1, :]) / jnp.maximum(jnp.sum(totals[1:2, :]), 1e-30)
+    with jax.named_scope("prepare"):
+        lax.fori_loop(0, count // group, prepare, 0)
+
+    filled = jnp.sum(occ_all[...].astype(jnp.float32), axis=1, keepdims=True) / wide
+    sigma = coupling * jnp.sum(filled * filled)
     sigma_out[...] = jnp.full((8, tile), sigma, jnp.float32)
 
     def shifted(left, store):
@@ -434,7 +413,7 @@
         lax.fori_loop(0, count, one, 0, unroll=2)
 
     for h in range(2):
-        arrive(up_in(vt, x2, p_send, p_recv, h, True))
+        arrive(f"wait_x2_{h}", up_in(vt, x2, p_send, p_recv, h, True))
         load_columns(x2, vt, h)
         hop()
         finish(keep_columns(u2, u0, h))
@@ -442,8 +421,9 @@
         shifted(cols_t[subs(h * half + me_up * piece, piece), :], y)
         run([pltpu.make_async_copy(y, g2.at[h], local.at[0])])
 
+    behind = []
     for c in range(2):
-        arrive(z_in(c, True))
+        arrive(f"wait_x1_{c}", z_in(c, True))
         load_rows(c)
         hop()
         finish(keep_rows(dn1, d0, c))
@@ -451,21 +431,24 @@
             launch(z_out(dn1, d0, b_send, b_recv, halves[0], 0, 0, False))
         else:
             launch(z_out(dn1, d0, b_send, b_recv, halves[0], 0, 1, False))
-            launch(z_out(dn1, d0, b_send, b_recv, halves[1], 1, 0, False))
-            launch(z_out(dn1, d0, b_send, b_recv, halves[1], 1, 1, False))
+            for part in range(2):
+                late = z_out(dn1, d0, b_send, b_recv, halves[1], 1, part, False)
+                for copy in late:
+                    copy.start()
+                behind.extend(late)
         shifted(rows_t[subs(me_dn * 2 * piece + c * piece, piece), :], x)
         hop()
         finish(keep_rows(s1, s0, c))
 
     def flip(h):
         for c in range(2):
-            arrive(z_out(dn1, d0, b_send, b_recv, halves[h], h, c, True))
+            arrive(f"wait_d0_{h}", z_out(dn1, d0, b_send, b_recv, halves[h], h, c, True))
         run([pltpu.make_async_copy(d0.at[pl.ds(h * half_tiles, half_tiles)], a, local.at[0])])
-        turn(dt, h, nothing)
+        turn(dt, h)
         launch(up_in(dt, d2, t_send, t_recv, h, False))
 
     def second(h):
-        arrive(up_in(dt, d2, t_send, t_recv, h, True))
+        arrive(f"wait_d2_{h}", up_in(dt, d2, t_send, t_recv, h, True))
         load_columns(d2, dt, h)
         run([pltpu.make_async_copy(g2.at[h], y, local.at[0])])
 
@@ -480,10 +463,13 @@
         launch(up_out(r2, r0, o_send, o_recv, h, False))
 
     flip(0)
+    second(0)
+    with jax.named_scope("wait_behind"):
+        for copy in behind:
+            copy.wait_send()
     for slot, span in enumerate(spans):
         for c in range(2):
             launch(z_out(s1, s0, c_send, c_recv, span, slot, c, False))
-    second(0)
     flip(1)
     second(1)
 
@@ -538,7 +524,7 @@
                 pairs = (m * m, m * total, m * value, total * total, total * value, value * value)
                 return tuple(c + fold(p) for c, p in zip(carry, pairs))
 
-            carry = lax.fori_loop(0, tall_tiles, block, carry)
+            carry = lax.fori_loop(0, tall_tiles, block, carry, unroll=True)
             for copy in strip_out(i, slot):
                 copy.start()
             return carry
@@ -549,20 +535,24 @@
         return carry
 
     carry = tuple(jnp.zeros((8, tile), jnp.float32) for _ in range(6))
-    for h in range(2):
-        arrive(up_out(u2, u0, q_send, q_recv, h, True))
-        arrive(up_out(r2, r0, o_send, o_recv, h, True))
     for slot, span in enumerate(spans):
+        if span[0] in (0, half_tiles):
+            arrive("wait_u0", up_out(u2, u0, q_send, q_recv, min(slot, 1), True))
+            arrive("wait_r0", up_out(r2, r0, o_send, o_recv, min(slot, 1), True))
         for c in range(2):
-            arrive(z_out(s1, s0, c_send, c_recv, span, slot, c, True))
-        carry = combine(span[0], span[1], carry)
+            arrive(f"wait_s0_{slot}", z_out(s1, s0, c_send, c_recv, span, slot, c, True))
+        with jax.named_scope(f"combine_{slot}"):
+            carry = combine(span[0], span[1], carry)
+    row = lax.broadcasted_iota(jnp.int32, (8, tile), 0)
     packed = jnp.zeros((8, tile), jnp.float32)
     for k in range(6):
         packed = jnp.where(row == k, jnp.sum(carry[k], axis=0, keepdims=True), packed)
     last[...] = packed
-    gram_out[...] = reduce_all(n_up, n_dn, me_up, me_dn, last, z_last, up_last, last_sems)
-    for copy in started:
-        copy.wait_send()
+    with jax.named_scope("reduce_last"):
+        gram_out[...] = reduce_all(n_up, n_dn, me_up, me_dn, last, z_last, up_last, last_sems)
+    with jax.named_scope("drain"):
+        for copy in started:
+            copy.wait_send()
 
 
 def exchange(v, tiles, columns, signs, occ_all, occ_mine, rows_t, cols_t):
@@ -606,9 +596,6 @@
             pltpu.VMEM((2, 2, tall, tile, tile), bf16),
             pltpu.VMEM((2, 2, rows, tile), bf16),
             pltpu.VMEM((8, tile), f32),
-            pltpu.VMEM((8, tile), f32),
-            pltpu.VMEM((n_dn, 8, tile), f32),
-            pltpu.VMEM((n_up, 8, tile), f32),
             pltpu.VMEM((n_dn, 8, tile), f32),
             pltpu.VMEM((n_up, 8, tile), f32),
             dma((max(n_up, n_dn),)),
@@ -616,7 +603,7 @@
             dma((2, 5)),
             dma((2, 2)),
             dma((2, n_dn - 1)), dma((2, n_dn)),
-            *z4, *zs, *up2, *up2, *up2, *up2, sums, sums,
+            *z4, *zs, *up2, *up2, *up2, *up2, sums,
         ],
         compiler_params=pltpu.CompilerParams(
             collective_id=0, has_side_effects=True, vmem_limit_bytes=60 * 1024 * 1024
@@ -628,7 +615,7 @@
     return outs[:4]
 
 
-def final_kernel(m, w, v, sigma, gram, out, scalars):
+def final_scalars(sigma, gram):
     mm, mw, mv, ww, wv, vv = (jnp.sum(gram[k : k + 1, :], axis=1, keepdims=True) for k in range(6))
     shift = sigma[0:1, 0:1]
     scale = 1.0 / jnp.maximum(jnp.sqrt(vv), 1.0)
@@ -647,24 +634,35 @@
     residual = mm + c1 * c1 * ww + c2 * c2 * vv + 2.0 * (c1 * mw + c2 * mv + c1 * c2 * wv)
     beta2 = jnp.sqrt(jnp.maximum(gain * residual, 1.0))
     factor = scale / (beta1 * beta2)
-    value = m[0].astype(jnp.float32) + c1 * w[0].astype(jnp.float32) + c2 * v[...].astype(jnp.float32)
-    out[...] = (factor * value).astype(jnp.bfloat16)
-    row = lax.broadcasted_iota(jnp.int32, scalars.shape, 0)
-    found = jnp.zeros(scalars.shape, jnp.float32)
-    for k, value in enumerate((alpha1, alpha2, beta1, beta2)):
-        found = jnp.where(row == k, value, found)
-    scalars[...] = found
+    return alpha1, alpha2, beta1, beta2, factor, factor * c1, factor * c2
+
+
+def final_kernel(m, w, v, sigma, gram, out, scalars):
+    @pl.when(pl.program_id(0) == 0)
+    def _():
+        row = lax.broadcasted_iota(jnp.int32, scalars.shape, 0)
+        found = jnp.zeros(scalars.shape, jnp.float32)
+        for k, value in enumerate(final_scalars(sigma, gram)):
+            found = jnp.where(row == k, value, found)
+        scalars[...] = found
+
+    factor, c1, c2 = scalars[4:5, :], scalars[5:6, :], scalars[6:7, :]
+    tile = m.shape[2]
+    for k in range(m.shape[0]):
+        at = slice(k * tile, (k + 1) * tile)
+        value = factor * m[k].astype(jnp.float32) + c1 * w[k].astype(jnp.float32)
+        out[:, at] = (value + c2 * v[:, at].astype(jnp.float32)).astype(jnp.bfloat16)
 
 
 def finish_all(m, w, v, sigma, gram):
     rows, cols = v.shape
     tile = m.shape[2]
-    column = pl.BlockSpec((rows, tile), lambda i: (0, i))
-    strip = pl.BlockSpec((1, rows, tile), lambda i: (i, 0, 0))
+    column = pl.BlockSpec((tile, cols), lambda i: (i, 0))
+    strip = pl.BlockSpec((cols // tile, tile, tile), lambda i: (0, i, 0))
     small = pl.BlockSpec((8, tile), lambda i: (0, 0))
     return pl.pallas_call(
         final_kernel,
-        grid=(cols // tile,),
+        grid=(rows // tile,),
         in_specs=[strip, strip, column, small, small],
         out_specs=[column, small],
         out_shape=[

time: 942 us -> 771 us (0.82)
  Pallas kernels: 932 us -> 761 us
    pallas_call x1, Pallas kernels: 904 us -> 741 us  [exchange(): pl.pallas_call(functools.partial(kernel, (n_up, n_dn, count, tile_k, tile...]
where the time goes in v2:
time: 771 us; the launch traced here: 770 us
  Pallas kernels  761 us (99%)
    pallas_call x1, Pallas kernels, exchange(): pl.pallas_call(functools.partial(kernel, (n_up, n_dn, count, tile_k, tile...  741 us
    pallas_call x1, Pallas kernels, finish_all(): pl.pallas_call(final_kernel, grid=(rows // tile,), in_specs=[strip, strip...  20.5 us

profile of v2, /device:TPU:0, one launch (start us, length us, event | category | flops | bytes accessed | tf_op | source)
XLA Modules:
  0.0 769.8 jit_solution(9934300218106609189)
XLA Ops:
  0.6 0.8 copy.16
  1.4 0.8 reshape.12.columns
  2.2 0.8 copy.17
  3.0 0.8 reshape.13.signs
  3.8 1.2 convert_element_type.3.occ_all
  5.0 0.0 copy-start
  5.0 0.0 copy-start.1
  5.0 1.0 copy.22
  6.0 1.2 copy.21
  7.2 0.0 copy-done
  7.2 0.0 copy-done.1
  7.2 740.7 %shard_map.76 = (bf16[26,1664,128]{2,1,0:T(8,128)(2,1)}, bf16[26,1664,128]{2,1,0:T(8,128)(2,1)}, f32[8,128]{1,0:T(8,128)}, f32[8,128]{1,0:T(8,128)}, bf16[26,166...) custom-call(s32[520]{0:T(1024)} %reshape.12.columns, ...), custom_call_target="tpu_custom_call" | custom-call | flops 28353495040 | bytes 332267520 | tf_op jit(solution)/shard_map/pallas_call | solution.py:582
  747.9 20.5 %shard_map.77 = (bf16[1664,3328]{1,0:T(8,128)(2,1)}, f32[8,128]{1,0:T(8,128)}) custom-call(bf16[26,1664,128]{2,1,0:T(8,128)(2,1)} %get-tuple-element.9.m, bf16[26,1664,128]{2,1,0:T(8,128)(2,1)} %get-tuple-element.10.w, bf16[1664,3328]{1,0:T(8,128)(2,1)} %v.3, f32[8,128]{1,0:T(8,128)} %get-tuple-element.11.sigma, f32[8,128]{1,0:T(8,128)} %get-tuple-element.12.gram), custom_call_target="tpu_custom_call" | custom-call | tf_op jit(solution)/shard_map/pallas_call | solution.py:663
  768.4 1.4 slice_reduce_fusion
  (2 shorter events, 0.0 us)
Async XLA Ops:
  5.0 2.3 copy-start
  5.0 2.2 copy-start.1
